TPU v7x, 32 devices: a whole 2x2x4 slice. The times are simulated.
32 devices in a mesh: dp: 2 (over y), seq: 16 (over z, x, core).
Axes of the slice: x: 2, y: 2, z: 4, core: 2. Of those that a mesh axis runs over, the one named last changes fastest.
Arguments:
- features: bfloat16 [4096, 320], P(('dp', 'seq')), parts along dimension 0, may hold values from -40 to 40
- hint: bfloat16 [4096, 320], P(('dp', 'seq')), parts along dimension 0, may hold values from -6 to 6
- conv_weight: bfloat16 [3, 3, 320, 320], replicated, may hold values from -0.109375 to 0.109375
- conv_bias: float32 [320], replicated, may hold values from -3 to 3
- zero_weight: bfloat16 [320, 320], replicated, may hold values from -0.3125 to 0.3125
- zero_bias: float32 [320], replicated, may hold values from -2 to 2
- group_gain: float32 [320], replicated, may hold values from 0.5 to 1.5
- proj_in: bfloat16 [320, 320], replicated, may hold values from -0.3125 to 0.3125
- norm_gain: float32 [320], replicated, may hold values from 0.5 to 1.5
- query_weight: bfloat16 [320, 320], replicated, may hold values from -2 to 2
- key_weight: bfloat16 [320, 320], replicated, may hold values from -2 to 2
- value_weight: bfloat16 [320, 320], replicated, may hold values from -0.3125 to 0.3125
- attn_out: bfloat16 [320, 320], replicated, may hold values from -0.3125 to 0.3125
- proj_out: bfloat16 [320, 320], replicated, may hold values from -0.3125 to 0.3125
Outputs:
- block_out: bfloat16 [4096, 320], P(('dp', 'seq')), parts along dimension 0
There are 2 independent parts, one for each index of `dp`. A program takes and returns all parts, laid end to end along the dimension named above; an argument that names none is the same for every part. Nothing has to cross between parts.
All inputs are finite; a program needn't handle non-finite values.
Results may differ from a plain program's by a relative error of at most 0.023.
Values may be sent and summed in bfloat16 or wider, within the bound.
A program may use at most 64 MiB of HBM per device.

v0:
```python
import math

import jax
import jax.numpy as jnp
from jax import lax
from jax.sharding import PartitionSpec as P

HEADS = 8
GROUPS = 32
WIDTH = 128


norm_eps = 1e-06
layer_eps = 1e-05


def with_halo(block, sides, width):
    for axis, dim in sides:
        count = lax.axis_size(axis)
        forward = [(i, i + 1) for i in range(count - 1)]
        backward = [(target, source) for source, target in forward]
        low = lax.ppermute(
            lax.slice_in_dim(block, block.shape[dim] - width, None, axis=dim), axis, forward
        )
        high = lax.ppermute(lax.slice_in_dim(block, 0, width, axis=dim), axis, backward)
        block = jnp.concatenate([low, block, high], axis=dim)
    return block


def conv_extended(extended, conv_weight, conv_bias, width):
    line_count = extended.shape[0] // width - 2
    channels = extended.shape[1]
    lattice = extended.reshape(line_count + 2, width, channels)
    padded = jnp.pad(lattice, ((0, 0), (1, 1), (0, 0)))
    summed = jnp.zeros((line_count * width, conv_weight.shape[3]), jnp.float32)
    for row_shift in range(3):
        for col_shift in range(3):
            window = padded[row_shift : row_shift + line_count, col_shift : col_shift + width]
            window = window.reshape(line_count * width, channels)
            summed = summed + jnp.dot(
                window, conv_weight[row_shift, col_shift], preferred_element_type=jnp.float32
            )
    return summed + conv_bias


def fold_blocks(carry_in, queries, pieces, make_pairs):
    row_total = pieces[0].shape[0]
    block_len = math.gcd(row_total, 1024)
    stacked = tuple(
        (member.reshape(row_total // block_len, block_len, member.shape[1]) for member in pieces)
    )
    score_scale = 1.0 / math.sqrt(queries.shape[2])

    def advance(carry_now, slab_rows):
        running_max, running_sum, weighted = carry_now
        keys_block, values_block = make_pairs(slab_rows)
        scores = (
            jnp.einsum("qhd,khd->hqk", queries, keys_block, preferred_element_type=jnp.float32)
            * score_scale
        )
        new_max = jnp.maximum(running_max, jnp.max(scores, axis=2))
        decay_by = jnp.exp(running_max - new_max)
        weights = jnp.exp(scores - new_max[:, :, None])
        running_sum = running_sum * decay_by + jnp.sum(weights, axis=2)
        weighted = weighted * jnp.transpose(decay_by)[:, :, None] + jnp.einsum(
            "hqk,khd->qhd",
            weights.astype(jnp.bfloat16),
            values_block,
            preferred_element_type=jnp.float32,
        )
        return ((new_max, running_sum, weighted), None)

    carry_out, unused = lax.scan(advance, carry_in, stacked)
    return carry_out


def local(
    features,
    hint,
    conv_weight,
    conv_bias,
    zero_weight,
    zero_bias,
    group_gain,
    proj_in,
    norm_gain,
    query_weight,
    key_weight,
    value_weight,
    attn_out,
    proj_out,
):
    tok_count, channels = features.shape
    head_dim = channels // HEADS
    extended = with_halo(hint, (("seq", 0),), WIDTH)
    control = jax.nn.silu(conv_extended(extended, conv_weight, conv_bias, WIDTH)).astype(
        jnp.bfloat16
    )
    branch = jnp.dot(control, zero_weight, preferred_element_type=jnp.float32) + zero_bias
    merged = (features.astype(jnp.float32) + branch).astype(jnp.bfloat16)
    widened = merged.astype(jnp.float32)
    per_group = channels // GROUPS
    entry_count = tok_count * lax.axis_size("seq") * per_group
    local_sum = jnp.sum(widened.reshape(tok_count, GROUPS, per_group), axis=(0, 2))
    mean_group = lax.psum(local_sum, "seq") / entry_count
    centred = widened - jnp.repeat(mean_group, per_group)
    local_spread = jnp.sum(jnp.square(centred).reshape(tok_count, GROUPS, per_group), axis=(0, 2))
    var_group = lax.psum(local_spread, "seq") / entry_count
    mean_chan = jnp.repeat(mean_group, per_group)
    inv_chan = jnp.repeat(lax.rsqrt(var_group + norm_eps), per_group)
    grouped = ((widened - mean_chan) * inv_chan * group_gain).astype(jnp.bfloat16)
    inner_rows = jnp.dot(grouped, proj_in, preferred_element_type=jnp.float32).astype(jnp.bfloat16)
    inner_wide = inner_rows.astype(jnp.float32)
    centre = jnp.mean(inner_wide, axis=1, keepdims=True)
    spread = jnp.mean(jnp.square(inner_wide - centre), axis=1, keepdims=True)
    normed = ((inner_wide - centre) * lax.rsqrt(spread + layer_eps) * norm_gain).astype(
        jnp.bfloat16
    )
    queries = jnp.dot(normed, query_weight, preferred_element_type=jnp.float32).astype(jnp.bfloat16)
    queries = queries.reshape(tok_count, HEADS, head_dim)
    group_span = lax.axis_size("seq") // HEADS
    sub_rows = tok_count // group_span
    local_keys = jnp.dot(normed, key_weight, preferred_element_type=jnp.float32).astype(
        jnp.bfloat16
    )
    local_values = jnp.dot(normed, value_weight, preferred_element_type=jnp.float32).astype(
        jnp.bfloat16
    )
    query_send = (
        queries.reshape(group_span, sub_rows, HEADS, head_dim)
        .transpose(2, 0, 1, 3)
        .reshape(HEADS * group_span, sub_rows, head_dim)
    )

    def copies_for(matrix):
        by_head = matrix.reshape(tok_count, HEADS, head_dim).transpose(1, 0, 2)
        return jnp.broadcast_to(by_head[:, None], (HEADS, group_span, tok_count, head_dim)).reshape(
            HEADS * group_span, tok_count, head_dim
        )

    own_queries = lax.all_to_all(query_send, "seq", split_axis=0, concat_axis=0, tiled=True)
    head_keys, head_values = (
        lax.all_to_all(copies_for(local_keys), "seq", split_axis=0, concat_axis=0, tiled=True),
        lax.all_to_all(copies_for(local_values), "seq", split_axis=0, concat_axis=0, tiled=True),
    )
    query_rows = own_queries.shape[0] * sub_rows
    own_queries = own_queries.reshape(query_rows, 1, head_dim)
    key_rows = head_keys.reshape(-1, head_dim)
    value_rows = head_values.reshape(-1, head_dim)

    def single_pairs(slab_rows):
        return (slab_rows[0].reshape(-1, 1, head_dim), slab_rows[1].reshape(-1, 1, head_dim))

    head_carry = (
        jnp.full((1, query_rows), -1e30, jnp.float32),
        jnp.zeros((1, query_rows), jnp.float32),
        jnp.zeros((query_rows, 1, head_dim), jnp.float32),
    )
    running_max, running_sum, weighted = fold_blocks(
        head_carry, own_queries, (key_rows, value_rows), single_pairs
    )
    head_result = (weighted / jnp.transpose(running_sum)[:, :, None]).astype(jnp.bfloat16)
    head_result = head_result.reshape(lax.axis_size("seq"), sub_rows, head_dim)
    returned = lax.all_to_all(head_result, "seq", split_axis=0, concat_axis=0, tiled=True)
    attended = (
        returned.reshape(HEADS, group_span, sub_rows, head_dim)
        .transpose(1, 2, 0, 3)
        .reshape(tok_count, channels)
    )
    after_attn = (
        inner_wide + jnp.dot(attended, attn_out, preferred_element_type=jnp.float32)
    ).astype(jnp.bfloat16)
    return (widened + jnp.dot(after_attn, proj_out, preferred_element_type=jnp.float32)).astype(
        jnp.bfloat16
    )


def solution(mesh):
    placed = (
        P(("dp", "seq"), None),
        P(("dp", "seq"), None),
        P(),
        P(),
        P(),
        P(),
        P(),
        P(),
        P(),
        P(),
        P(),
        P(),
        P(),
        P(),
    )
    return jax.shard_map(
        local, mesh=mesh, in_specs=placed, out_specs=P(("dp", "seq"), None), check_vma=False
    )
```

profile of v0, /device:TPU:0, one launch (start us, length us, event | category | flops | bytes accessed | tf_op | source)
XLA Modules:
  0.0 143.6 jit_solution(5059006337217862261)
XLA Ops:
  0.0 2.7 %collective-permute-start = (bf16[128,320]{0,1:T(8,128)(2,1)}, bf16[128,320]{0,1:T(8,128)(2,1)S(1)}, u32[]{:S(2)}, u32[]{:S(2)}) collective-permute-start(bf16[128,320]{0,1:T(8,128)(2,1)} %param.17), channel_id=1, source_target_pairs={{0,1},{1,2},{2,3},{3,4},{4,5},{5,6},{6,7},{7,8},{8,9},{9,10},{10,1... | collective-permute-start | bytes 245768 | tf_op jit(solution)/shard_map/ppermute | solution.py:22
  2.7 1.3 collective-permute-start.1
  4.0 4.2 %collective-permute-done.1 = bf16[128,320]{0,1:T(8,128)(2,1)S(1)} collective-permute-done((bf16[128,320]{0,1:T(8,128)(2,1)}, bf16[128,320]{0,1:T(8,128)(2,1)S(1)}, u32[]{:S(2)}, u32[]{:S(2)}) %collective-permute-start.1) | collective-permute-done | bytes 81952 | tf_op jit(solution)/shard_map/ppermute | solution.py:25
  8.1 1.0 pad_maximum_fusion
  9.1 0.2 copy.64
  9.3 1.2 fusion.39
  10.6 1.9 %fusion.30 = f32[128,320]{0,1:T(8,128)} fusion(bf16[3,3,320,320]{3,2,1,0:T(8,128)(2,1)} %param.18, bf16[3,128,320]{2,1,0:T(8,128)(2,1)S(1)} %bitcast.143), kind=kOutput, calls=%fused_computation.46 | convolution fusion | flops 26214400 | bytes 655360 | tf_op jit(solution)/shard_map/dot_general | solution.py:40
  12.5 0.3 convolution_add_fusion.9
  12.8 0.3 convolution_add_fusion.8
  13.1 0.3 convolution_add_fusion.7
  13.4 0.3 convolution_add_fusion.6
  13.7 0.3 convolution_add_fusion.5
  14.0 0.9 convolution_add_fusion.4
  15.0 1.7 %fusion.78 = (f32[320]{0:T(512)S(1)}, f32[128,320]{0,1:T(8,128)S(1)}) fusion(f32[320]{0:T(512)S(1)} %copy-done.13, bf16[320,320]{1,0:T(8,128)(2,1)S(1)} %copy-done, f32[128,320]{0,1:T(8,128)} %fusion.30, f32[128,320]{0,1:T(8,128)} %convolution_add_fusion.4, bf16[128,320]{0,1:T(8,128)(2,1)} %copy-done.10, bf16[3,3,320,320]{3,2,1,0:T(8,128)(2,1)S(1)} %copy-done.2, ...), kind=kOutput, calls=%fused_computation.100 | convolution fusion | flops 53001920 | bytes 1152256 | tf_op jit(solution)/shard_map/dot_general | solution.py:99
  16.9 32.7 %psum.14 = f32[32]{0:T(128)S(1)} all-reduce(f32[32]{0:T(128)S(1)} %reduce_sum.63), channel_id=1, replica_groups=mesh['dp'=2,'seq'=16] {'seq'}, use_global_device_ids=true, to_apply=%region_2.3 | all-reduce | flops 32 | bytes 256 | tf_op jit(solution)/shard_map/psum | solution.py:105
  49.8 0.2 multiply_reduce_fusion.2
  50.2 29.5 %psum.15 = f32[32]{0:T(128)S(1)} all-reduce(f32[32]{0:T(128)S(1)} %reduce_sum.66), channel_id=1, replica_groups=mesh['dp'=2,'seq'=16] {'seq'}, use_global_device_ids=true, to_apply=%region_5.6 | all-reduce | flops 32 | bytes 256 | tf_op jit(solution)/shard_map/psum | solution.py:108
  80.0 0.5 fusion.81
  80.7 0.3 convolution_convert_fusion.1
  81.1 0.8 reshape.134
  81.9 3.5 %all-to-all-start.1 = ((bf16[16,2,1280]{2,1,0:T(2,128)(2,1)}), bf16[16,2,1280]{2,1,0:T(2,128)(2,1)S(1)}, u32[]{:S(2)}, u32[]{:S(2)}) async-start(bf16[16,2,1280]{2,1,0:T(2,128)(2,1)} %reshape.134), calls=%async_computation.1 | async-start | bytes 163840 | tf_op jit(solution)/shard_map/all_to_all | solution.py:141
  85.4 0.3 convolution_convert_fusion.2
  85.7 6.8 %all-to-all-done.1 = bf16[16,2,1280]{2,1,0:T(2,128)(2,1)S(1)} async-done(((bf16[16,2,1280]{2,1,0:T(2,128)(2,1)}), bf16[16,2,1280]{2,1,0:T(2,128)(2,1)S(1)}, u32[]{:S(2)}, u32[]{:S(2)}) %all-to-all-start.1) | async-done | bytes 81952 | tf_op jit(solution)/shard_map/all_to_all | solution.py:141
  92.5 0.7 broadcast_in_dim.19
  93.2 3.5 %all-to-all-start = ((bf16[16,128,40]{1,2,0:T(8,128)(2,1)}), bf16[16,128,40]{1,2,0:T(8,128)(2,1)S(1)}, u32[]{:S(2)}, u32[]{:S(2)}) async-start(bf16[16,128,40]{1,2,0:T(8,128)(2,1)} %bitcast.18), calls=%async_computation | async-start | bytes 327680 | tf_op jit(solution)/shard_map/all_to_all | solution.py:143
  96.7 0.3 convolution_convert_fusion
  97.0 8.1 %all-to-all-done = bf16[16,128,40]{1,2,0:T(8,128)(2,1)S(1)} async-done(((bf16[16,128,40]{1,2,0:T(8,128)(2,1)}), bf16[16,128,40]{1,2,0:T(8,128)(2,1)S(1)}, u32[]{:S(2)}, u32[]{:S(2)}) %all-to-all-start) | async-done | bytes 163872 | tf_op jit(solution)/shard_map/all_to_all | solution.py:143
  105.1 0.7 broadcast_in_dim.20
  105.8 3.5 %all-to-all-start.2 = ((bf16[16,128,40]{1,2,0:T(8,128)(2,1)}), bf16[16,128,40]{1,2,0:T(8,128)(2,1)S(1)}, u32[]{:S(2)}, u32[]{:S(2)}) async-start(bf16[16,128,40]{1,2,0:T(8,128)(2,1)} %bitcast.24), calls=%async_computation.2 | async-start | bytes 327680 | tf_op jit(solution)/shard_map/all_to_all | solution.py:144
  109.3 0.2 reshape.135
  109.5 0.2 reshape.125
  109.7 0.3 copy.79
  110.0 7.7 %all-to-all-done.2 = bf16[16,128,40]{1,2,0:T(8,128)(2,1)S(1)} async-done(((bf16[16,128,40]{1,2,0:T(8,128)(2,1)}), bf16[16,128,40]{1,2,0:T(8,128)(2,1)S(1)}, u32[]{:S(2)}, u32[]{:S(2)}) %all-to-all-start.2) | async-done | bytes 163872 | tf_op jit(solution)/shard_map/all_to_all | solution.py:144
  117.7 0.3 copy.80
  118.0 13.9 %while.15 = (s32[]{:T(128)}, f32[1,1024]{1,0:T(1,128)S(1)}, f32[1,1024]{1,0:T(1,128)S(1)}, f32[1024,1,40]{0,2,1:T(8,128)S(1)}, bf16[2,1024,40]{2,1,0:T(8,128)(2,...) while((s32[]{:T(128)}, f32[1,1024]{1,0:T(1,128)S(1)}, ...), condition=%wide.region_11.12_spmd.clone, body=%wide.region_8.0_spmd.clone.sunk | while | flops 176288768 | bytes 30359692 | solution.py:73
  118.0 2.6 %multiply_reduce_fusion.4 = (f32[1024]{0:T(1024)S(1)}, f32[1024,1024]{1,0:T(8,128)}) fusion(bf16[1024,1,40]{0,2,1:T(8,128)(2,1)S(1)} %get-tuple-element.172, bf16[2,1024,40]{2,1,0:T(8,128)(2,1)S(1)} %get-tuple-element.171, s32[]{:T(128)} %get-tuple-element.158), kind=kOutput, calls=%fused_computation.1.clone.1 | convolution fusion | flops 85982208 | bytes 4542468 | tf_op jit(solution)/shard_map/while/body/eval_jaxpr/qhd,khd->hqk/dot_general | solution.py:58
  120.7 3.1 %fusion.105 = f32[1024]{0:T(1024)S(1)} fusion(f32[1024,1024]{1,0:T(8,128)} %get-tuple-element.146, f32[1024]{0:T(1024)S(1)} %bitcast.150), kind=kLoop, calls=%fused_computation.3.clone.1 | loop fusion | flops 3144704 | bytes 4202496 | tf_op jit(solution)/shard_map/while/body/eval_jaxpr/reduce_sum | solution.py:64
  123.8 0.3 copy-done.1
  124.1 0.8 fusion.107
  125.0 2.6 %multiply_reduce_fusion.4 = (f32[1024]{0:T(1024)S(1)}, f32[1024,1024]{1,0:T(8,128)}) fusion(bf16[1024,1,40]{0,2,1:T(8,128)(2,1)S(1)} %get-tuple-element.172, bf16[2,1024,40]{2,1,0:T(8,128)(2,1)S(1)} %get-tuple-element.171, s32[]{:T(128)} %get-tuple-element.158), kind=kOutput, calls=%fused_computation.1.clone.1 | convolution fusion | flops 85982208 | bytes 4542468 | tf_op jit(solution)/shard_map/while/body/eval_jaxpr/qhd,khd->hqk/dot_general | solution.py:58
  127.6 3.1 %fusion.105 = f32[1024]{0:T(1024)S(1)} fusion(f32[1024,1024]{1,0:T(8,128)} %get-tuple-element.146, f32[1024]{0:T(1024)S(1)} %bitcast.150), kind=kLoop, calls=%fused_computation.3.clone.1 | loop fusion | flops 3144704 | bytes 4202496 | tf_op jit(solution)/shard_map/while/body/eval_jaxpr/reduce_sum | solution.py:64
  130.7 0.3 copy-done.1
  131.0 0.8 fusion.107
  132.0 0.2 reshape.128
  132.2 0.2 reshape.136
  132.3 9.7 %all_to_all.20 = bf16[16,2,1280]{2,1,0:T(2,128)(2,1)S(1)} all-to-all(bf16[16,2,1280]{2,1,0:T(2,128)(2,1)S(1)} %reshape.136), channel_id=1, replica_groups=mesh['dp'=2,'seq'=16] {'seq'}, dimensions={0} | all-to-all | bytes 163840 | tf_op jit(solution)/shard_map/all_to_all | solution.py:164
  142.0 0.2 reshape.137
  142.5 1.1 fusion.28
  (61 shorter events, 1.6 us)
Async XLA Ops:
  0.0 15.0 %copy-start = (bf16[320,320]{1,0:T(8,128)(2,1)S(1)}, bf16[320,320]{1,0:T(8,128)(2,1)}, u32[]{:S(2)}) copy-start(bf16[320,320]{1,0:T(8,128)(2,1)} %param.20) | copy-start | bytes 614404
  0.0 12.5 %copy-start.2 = (bf16[3,3,320,320]{3,2,1,0:T(8,128)(2,1)S(1)}, bf16[3,3,320,320]{3,2,1,0:T(8,128)(2,1)}, u32[]{:S(2)}) copy-start(bf16[3,3,320,320]{3,2,1,0:T(8,128)(2,1)} %param.18) | copy-start | bytes 5529604
  0.0 4.0 %collective-permute-start = (bf16[128,320]{0,1:T(8,128)(2,1)}, bf16[128,320]{0,1:T(8,128)(2,1)S(1)}, u32[]{:S(2)}, u32[]{:S(2)}) collective-permute-start(bf16[128,320]{0,1:T(8,128)(2,1)} %param.17), channel_id=1, source_target_pairs={{0,1},{1,2},{2,3},{3,4},{4,5},{5,6},{6,7},{7,8},{8,9},{9,10},{10,1... | collective-permute-start | bytes 245768 | tf_op jit(solution)/shard_map/ppermute | solution.py:22
  2.7 5.5 %collective-permute-start.1 = (bf16[128,320]{0,1:T(8,128)(2,1)}, bf16[128,320]{0,1:T(8,128)(2,1)S(1)}, u32[]{:S(2)}, u32[]{:S(2)}) collective-permute-start(bf16[128,320]{0,1:T(8,128)(2,1)} %param.17), channel_id=1, source_target_pairs={{1,0},{2,1},{3,2},{4,3},{5,4},{6,5},{7,6},{8,7},{9,8},{10,9},{11,1... | collective-permute-start | bytes 245768 | tf_op jit(solution)/shard_map/ppermute | solution.py:25
  8.1 1.2 copy-start.10
  9.1 4.3 %copy-start.3 = (bf16[128,320]{0,1:T(8,128)(2,1)S(1)}, bf16[128,320]{0,1:T(8,128)(2,1)}, u32[]{:S(2)}) copy-start(bf16[128,320]{0,1:T(8,128)(2,1)} %param.17) | copy-start | bytes 245764
  12.8 2.2 %copy-start.13 = (f32[320]{0:T(512)S(1)}, f32[320]{0:T(512)}, u32[]{:S(2)}) copy-start(f32[320]{0:T(512)} %param.21) | copy-start | bytes 3844
  12.8 2.2 %copy-start.14 = (f32[320]{0:T(512)S(1)}, f32[320]{0:T(512)}, u32[]{:S(2)}) copy-start(f32[320]{0:T(512)} %param.19) | copy-start | bytes 3844
  13.4 66.6 %copy-start.4 = (bf16[320,320]{1,0:T(8,128)(2,1)S(1)}, bf16[320,320]{1,0:T(8,128)(2,1)}, u32[]{:S(2)}) copy-start(bf16[320,320]{1,0:T(8,128)(2,1)} %param.23) | copy-start | bytes 614404
  13.4 66.6 %copy-start.11 = (f32[320]{0:T(512)S(1)}, f32[320]{0:T(512)}, u32[]{:S(2)}) copy-start(f32[320]{0:T(512)} %param.22) | copy-start | bytes 3844
  13.7 66.8 %copy-start.12 = (f32[320]{0:T(512)S(1)}, f32[320]{0:T(512)}, u32[]{:S(2)}) copy-start(f32[320]{0:T(512)} %param.24) | copy-start | bytes 3844
  13.7 66.9 %copy-start.5 = (bf16[320,320]{1,0:T(8,128)(2,1)S(1)}, bf16[320,320]{1,0:T(8,128)(2,1)}, u32[]{:S(2)}) copy-start(bf16[320,320]{1,0:T(8,128)(2,1)} %param.25) | copy-start | bytes 614404
  15.0 70.5 %copy-start.6 = (bf16[320,320]{1,0:T(8,128)(2,1)S(1)}, bf16[320,320]{1,0:T(8,128)(2,1)}, u32[]{:S(2)}) copy-start(bf16[320,320]{1,0:T(8,128)(2,1)} %param.26) | copy-start | bytes 614404
  16.7 80.0 %copy-start.7 = (bf16[320,320]{1,0:T(8,128)(2,1)S(1)}, bf16[320,320]{1,0:T(8,128)(2,1)}, u32[]{:S(2)}) copy-start(bf16[320,320]{1,0:T(8,128)(2,1)} %param.27) | copy-start | bytes 614404
  81.9 10.6 %all-to-all-start.1 = ((bf16[16,2,1280]{2,1,0:T(2,128)(2,1)}), bf16[16,2,1280]{2,1,0:T(2,128)(2,1)S(1)}, u32[]{:S(2)}, u32[]{:S(2)}) async-start(bf16[16,2,1280]{2,1,0:T(2,128)(2,1)} %reshape.134), calls=%async_computation.1 | async-start | bytes 163840 | tf_op jit(solution)/shard_map/all_to_all | solution.py:141
  93.2 11.9 %all-to-all-start = ((bf16[16,128,40]{1,2,0:T(8,128)(2,1)}), bf16[16,128,40]{1,2,0:T(8,128)(2,1)S(1)}, u32[]{:S(2)}, u32[]{:S(2)}) async-start(bf16[16,128,40]{1,2,0:T(8,128)(2,1)} %bitcast.18), calls=%async_computation | async-start | bytes 327680 | tf_op jit(solution)/shard_map/all_to_all | solution.py:143
  105.8 11.9 %all-to-all-start.2 = ((bf16[16,128,40]{1,2,0:T(8,128)(2,1)}), bf16[16,128,40]{1,2,0:T(8,128)(2,1)S(1)}, u32[]{:S(2)}, u32[]{:S(2)}) async-start(bf16[16,128,40]{1,2,0:T(8,128)(2,1)} %bitcast.24), calls=%async_computation.2 | async-start | bytes 327680 | tf_op jit(solution)/shard_map/all_to_all | solution.py:144
  120.7 3.4 %copy-start.1 = (f32[1024,1024]{1,0:T(8,128)S(1)}, f32[1024,1024]{1,0:T(8,128)}, u32[]{:S(2)}) copy-start(f32[1024,1024]{1,0:T(8,128)} %get-tuple-element.146) | copy-start | bytes 12582916 | tf_op jit(solution)/shard_map/while
  127.6 3.4 %copy-start.1 = (f32[1024,1024]{1,0:T(8,128)S(1)}, f32[1024,1024]{1,0:T(8,128)}, u32[]{:S(2)}) copy-start(f32[1024,1024]{1,0:T(8,128)} %get-tuple-element.146) | copy-start | bytes 12582916 | tf_op jit(solution)/shard_map/while
  131.9 10.6 %copy-start.8 = (bf16[320,320]{1,0:T(8,128)(2,1)S(1)}, bf16[320,320]{1,0:T(8,128)(2,1)}, u32[]{:S(2)}) copy-start(bf16[320,320]{1,0:T(8,128)(2,1)} %param.29) | copy-start | bytes 614404
  131.9 10.6 %copy-start.9 = (bf16[320,320]{1,0:T(8,128)(2,1)S(1)}, bf16[320,320]{1,0:T(8,128)(2,1)}, u32[]{:S(2)}) copy-start(bf16[320,320]{1,0:T(8,128)(2,1)} %param.28) | copy-start | bytes 614404
where the time goes:
time: 144 us
  blocking collectives  71.9 us (50%)
  waiting for transfers between devices  26.7 us (19%)
  matrix products  16.6 us (12%)
  starting transfers between devices  14.5 us (10%)
  other arithmetic  7.84 us (5%)
  local copies, waits for them, and re-layouts  5.58 us (4%)
    psum x1, blocking collectives, local(): mean_group = lax.psum(local_sum, 'seq') / entry_count  32.7 us
    psum x1, blocking collectives, local(): var_group = lax.psum(local_spread, 'seq') / entry_count  29.5 us
    all_to_all x1, blocking collectives, local(): lax.all_to_all(head_result, 'seq', split_axis=0, concat_axis=0, tiled=True)  9.7 us
    all_to_all x1, waiting for transfers between devices, local(): lax.all_to_all(copies_for(local_keys), 'seq', split_axis=0, concat_axis=0...  8.08 us
    all_to_all x1, waiting for transfers between devices, local(): lax.all_to_all(copies_for(local_values), 'seq', split_axis=0, concat_axis...  7.68 us
    all_to_all x1, waiting for transfers between devices, local(): lax.all_to_all(query_send, 'seq', split_axis=0, concat_axis=0, tiled=True)  6.76 us
    reduce_sum x2, other arithmetic, advance(): running_sum = running_sum * decay_by + jnp.sum(weights, axis=2)  6.15 us
    dot_general x8, matrix products, conv_extended(): jnp.dot(window, conv_weight[row_shift, col_shift], preferred_element_type...  5.47 us
  transfers between devices with their start and end apart: 5, of which 4 were waited for; matrix products, arithmetic and copies ran while one was open for 1% of the time, Pallas kernels for 0%

commit v1 on v0

v1 whole, which is shorter than its diff:
```python
import functools
import math

import jax
import jax.numpy as jnp
from jax import lax
from jax.experimental import pallas as pl
from jax.experimental.pallas import tpu as pltpu
from jax.sharding import PartitionSpec as P

HEADS = 8
GROUPS = 32
WIDTH = 128
CORES = 2

norm_eps = 1e-06
layer_eps = 1e-05
MESH = pl.DeviceIdType.MESH
F32 = jnp.float32
BF16 = jnp.bfloat16


def mm(x, y):
    return jnp.dot(x, y, preferred_element_type=F32)


def block_kernel(
    n, rows_a, rows_b,
    features, hint, conv_bias, zero_bias, group_gain, norm_gain,
    conv_hbm, zero_hbm, proj_in_hbm, query_hbm, key_hbm, value_hbm, attn_hbm, proj_hbm,
    out,
    conv_w, zero_w, proj_in_w, query_w, key_w, value_w, attn_w, proj_w,
    ext, gathered, normed_all, qmask, scores, mixed,
    load_sem, halo_send, halo_recv, send_sem, recv_sem,
):
    tokens, channels = features.shape
    head_dim = channels // HEADS
    per_group = channels // GROUPS
    me = lax.axis_index("seq")
    core = lax.rem(me, CORES)
    chip = lax.div(me, CORES)
    b = lax.rem(chip, rows_b)
    a = lax.div(chip, rows_b)

    def device(aa, bb, cc):
        return (aa * rows_b + bb) * CORES + cc

    loads = {}
    for slot, (name, src, dst) in enumerate((
        ("conv", conv_hbm, conv_w), ("zero", zero_hbm, zero_w), ("proj_in", proj_in_hbm, proj_in_w),
        ("query", query_hbm, query_w), ("key", key_hbm, key_w), ("value", value_hbm, value_w),
        ("attn", attn_hbm, attn_w), ("proj", proj_hbm, proj_w),
    )):
        loads[name] = pltpu.make_async_copy(src, dst, load_sem.at[slot])
        loads[name].start()

    barrier = pltpu.get_barrier_semaphore()
    always = jnp.int32(1)
    peers = [
        (me > 0, me - 1), (me < n - 1, me + 1),
        (a > 0, device(a - 1, b, core)), (a < rows_a - 1, device(a + 1, b, core)),
        (None, device(a, b, 1 - core)),
    ]
    for k in range(1, rows_b):
        peers.append((None, device(a, lax.rem(b + k, rows_b), core)))
    count = jnp.int32(0)
    for cond, peer in peers:
        def greet(peer=peer):
            pl.semaphore_signal(barrier, inc=1, device_id={"seq": peer}, device_id_type=MESH)
        if cond is None:
            greet()
            count = count + always
        else:
            pl.when(cond)(greet)
            count = count + cond.astype(jnp.int32)
    pl.semaphore_wait(barrier, count)

    to_next = pltpu.make_async_remote_copy(
        hint.at[pl.ds(tokens - WIDTH, WIDTH)], ext.at[pl.ds(0, WIDTH)],
        halo_send.at[0], halo_recv.at[0], device_id={"seq": me + 1}, device_id_type=MESH)
    to_prev = pltpu.make_async_remote_copy(
        hint.at[pl.ds(0, WIDTH)], ext.at[pl.ds(WIDTH + tokens, WIDTH)],
        halo_send.at[1], halo_recv.at[1], device_id={"seq": me - 1}, device_id_type=MESH)
    pl.when(me < n - 1)(to_next.start)
    pl.when(me > 0)(to_prev.start)

    ext[pl.ds(WIDTH, tokens)] = hint[...]

    @pl.when(me == 0)
    def _():
        ext[pl.ds(0, WIDTH)] = jnp.zeros((WIDTH, channels), BF16)

    @pl.when(me == n - 1)
    def _():
        ext[pl.ds(WIDTH + tokens, WIDTH)] = jnp.zeros((WIDTH, channels), BF16)

    loads["conv"].wait()
    middle = hint[...]
    taps = [mm(middle, conv_w[1, d]) for d in range(3)]
    pl.when(me > 0)(to_next.wait_recv)
    pl.when(me < n - 1)(to_prev.wait_recv)
    for dy in (0, 2):
        lines = ext[pl.ds(dy * WIDTH, tokens)]
        taps = [taps[d] + mm(lines, conv_w[dy, d]) for d in range(3)]
    column = lax.rem(lax.broadcasted_iota(jnp.int32, (tokens, channels), 0), WIDTH)
    left = jnp.where(column == 0, 0.0, pltpu.roll(taps[0], 1, 0))
    right = jnp.where(column == WIDTH - 1, 0.0, pltpu.roll(taps[2], tokens - 1, 0))
    conv = left + taps[1] + right + conv_bias[...]
    control = (conv / (1.0 + jnp.exp(-conv))).astype(BF16)
    loads["zero"].wait()
    merged = (features[...].astype(F32) + (mm(control, zero_w[...]) + zero_bias[...])).astype(BF16)
    gathered[me] = merged

    pending = []

    def send(src, target, cond):
        slot = len(pending)
        copy = pltpu.make_async_remote_copy(
            gathered.at[src], gathered.at[src], send_sem.at[slot], recv_sem.at[src],
            device_id={"seq": target}, device_id_type=MESH)
        pending.append((cond, copy))
        if cond is None:
            copy.start()
        else:
            pl.when(cond)(copy.start)

    def arrive(src, cond):
        def wait():
            pltpu.make_async_remote_copy(
                gathered.at[src], gathered.at[src], send_sem.at[0], recv_sem.at[src],
                device_id={"seq": me}, device_id_type=MESH).wait_recv()
        if cond is None:
            wait()
        else:
            pl.when(cond)(wait)

    def spread(src, cond):
        for k in range(1, rows_b):
            send(src, device(a, lax.rem(b + k, rows_b), core), cond)
        send(src, device(a, b, 1 - core), cond)

    def cross(step):
        for k in range(1, rows_b):
            bb = lax.rem(b + k, rows_b)
            for sign in ((1,) if step == 0 else (-1, 1)):
                aa = a + sign * step
                cond = None if step == 0 else ((aa >= 0) & (aa < rows_a))
                src = device(aa, bb, core)
                arrive(src, cond)
                send(src, device(a, b, 1 - core), cond)

    send(me, device(a + 1, b, core), a < rows_a - 1)
    send(me, device(a - 1, b, core), a > 0)
    spread(me, None)
    for step in range(1, rows_a):
        low, high = device(a - step, b, core), device(a + step, b, core)
        has_low, has_high = a - step >= 0, a + step < rows_a
        arrive(low, has_low)
        send(low, device(a + 1, b, core), has_low & (a < rows_a - 1))
        spread(low, has_low)
        arrive(high, has_high)
        send(high, device(a - 1, b, core), has_high & (a > 0))
        spread(high, has_high)
        cross(step - 1)
    cross(rows_a - 1)
    for k in range(rows_a * rows_b):
        arrive(k * CORES + 1 - core, None)

    entry_count = tokens * n * per_group
    row_group = lax.div(lax.broadcasted_iota(jnp.int32, (channels, channels), 0), jnp.int32(per_group))
    col_group = lax.div(lax.broadcasted_iota(jnp.int32, (channels, channels), 1), jnp.int32(per_group))
    same = (row_group == col_group).astype(F32)

    def group_mean(partial):
        total = jnp.dot(partial, same, preferred_element_type=F32, precision=lax.Precision.HIGHEST)
        return jnp.sum(total, axis=0, keepdims=True) / entry_count

    def fold_rows(x):
        return jnp.sum(x.reshape(tokens // 8, 8, channels), axis=0)

    def add_sum(k, acc):
        return acc + fold_rows(gathered[k].astype(F32))

    zero_acc = jnp.zeros((8, channels), F32)
    mean = group_mean(lax.fori_loop(0, n, add_sum, zero_acc))

    def add_square(k, acc):
        return acc + fold_rows(jnp.square(gathered[k].astype(F32) - mean))

    var = group_mean(lax.fori_loop(0, n, add_square, zero_acc))
    inv = lax.rsqrt(var + norm_eps)
    gain = group_gain[...]
    loads["proj_in"].wait()

    def project_norm(block):
        grouped = ((block.astype(F32) - mean) * inv * gain).astype(BF16)
        inner = mm(grouped, proj_in_w[...]).astype(BF16)
        wide = inner.astype(F32)
        centred = wide - jnp.mean(wide, axis=1, keepdims=True)
        spread_row = jnp.mean(jnp.square(centred), axis=1, keepdims=True)
        return wide, (centred * lax.rsqrt(spread_row + layer_eps) * norm_gain[...]).astype(BF16)

    inner_own, normed_own = project_norm(merged)
    chunk = 4 if n % 4 == 0 else 1

    def norm_chunk(k, carry):
        block = gathered[pl.ds(k * chunk, chunk)].reshape(chunk * tokens, channels)
        normed_all[pl.ds(pl.multiple_of(k * chunk * tokens, chunk * tokens), chunk * tokens)] = project_norm(block)[1]
        return carry

    lax.fori_loop(0, n // chunk, norm_chunk, 0)

    loads["query"].wait()
    loads["key"].wait()
    queries = mm(normed_own, query_w[...])
    queries_t = jnp.transpose(queries)
    row_head = lax.div(lax.broadcasted_iota(jnp.int32, (channels, tokens), 0), jnp.int32(head_dim))
    for h in range(HEADS):
        qmask[:, h * tokens:(h + 1) * tokens] = jnp.where(row_head == h, queries_t, 0.0).astype(BF16)
    scale = math.log2(math.e) / math.sqrt(head_dim)
    qmask[...] = (mm(key_w[...], qmask[...]) * scale).astype(BF16)

    loads["value"].wait()
    value_t = jnp.transpose(value_w[...].astype(F32)).astype(BF16)
    pair = 2 * tokens
    keys = normed_all[...]
    for h2 in range(HEADS // 2):
        cols = slice(h2 * pair, (h2 + 1) * pair)
        scores[...] = mm(keys, qmask[:, cols])
        top = jnp.max(scores[...], axis=0, keepdims=True)
        weights = jnp.exp2(scores[...] - top)
        total = jnp.sum(weights, axis=0, keepdims=True)
        folded = lax.dot_general(keys, weights.astype(BF16), (((0,), (0,)), ((), ())),
                                 preferred_element_type=F32)
        folded = (folded / total).astype(BF16)
        values = mm(value_t, folded)
        for j in range(2):
            h = 2 * h2 + j
            mixed[pl.ds(h * head_dim, head_dim)] = values[h * head_dim:(h + 1) * head_dim, j * tokens:(j + 1) * tokens]
    attended = jnp.transpose(mixed[...]).astype(BF16)
    loads["attn"].wait()
    loads["proj"].wait()
    after = (inner_own + mm(attended, attn_w[...])).astype(BF16)
    out[...] = (merged.astype(F32) + mm(after, proj_w[...])).astype(BF16)

    pl.when(me < n - 1)(to_next.wait_send)
    pl.when(me > 0)(to_prev.wait_send)
    for cond, copy in pending:
        if cond is None:
            copy.wait_send()
        else:
            pl.when(cond)(copy.wait_send)


def local(
    n, features, hint, conv_weight, conv_bias, zero_weight, zero_bias, group_gain, proj_in,
    norm_gain, query_weight, key_weight, value_weight, attn_out, proj_out,
):
    tokens, channels = features.shape
    chips = n // CORES
    rows_a = math.gcd(chips, 4)
    rows_b = chips // rows_a
    sends = 2 + rows_b + (rows_a - 1) * 2 * (1 + rows_b) + (2 * rows_a - 1) * (rows_b - 1)
    square = pltpu.VMEM((channels, channels), BF16)
    vmem = pl.BlockSpec(memory_space=pltpu.VMEM)
    hbm = pl.BlockSpec(memory_space=pl.ANY)
    row = lambda v: v.reshape(1, channels)
    return pl.pallas_call(
        functools.partial(block_kernel, n, rows_a, rows_b),
        out_shape=jax.ShapeDtypeStruct((tokens, channels), BF16),
        in_specs=[vmem] * 6 + [hbm] * 8,
        out_specs=vmem,
        scratch_shapes=[
            pltpu.VMEM(conv_weight.shape, BF16), square, square, square, square, square, square, square,
            pltpu.VMEM((tokens + 2 * WIDTH, channels), BF16),
            pltpu.VMEM((n, tokens, channels), BF16),
            pltpu.VMEM((n * tokens, channels), BF16),
            pltpu.VMEM((channels, HEADS * tokens), BF16),
            pltpu.VMEM((n * tokens, 2 * tokens), F32),
            pltpu.VMEM((channels, tokens), F32),
            pltpu.SemaphoreType.DMA((8,)),
            pltpu.SemaphoreType.DMA((2,)),
            pltpu.SemaphoreType.DMA((2,)),
            pltpu.SemaphoreType.DMA((sends,)),
            pltpu.SemaphoreType.DMA((n,)),
        ],
        compiler_params=pltpu.CompilerParams(
            collective_id=0, has_side_effects=True, vmem_limit_bytes=60 * 1024 * 1024),
    )(features, hint, row(conv_bias), row(zero_bias), row(group_gain), row(norm_gain),
      conv_weight, zero_weight, proj_in, query_weight, key_weight, value_weight, attn_out, proj_out)


def solution(mesh):
    split = P(("dp", "seq"), None)
    return jax.shard_map(
        functools.partial(local, mesh.shape["seq"]), mesh=mesh,
        in_specs=(split, split) + (P(),) * 12, out_specs=split, check_vma=False,
    )
```

time: 144 us -> 52.8 us (0.37)
  the two profiles are of different devices: /device:TPU:0 before, /device:TPU:3 now
where the time goes in v1:
time: 52.8 us; the launch traced here: 52.4 us
  Pallas kernels  42.5 us (80%)
  local copies, waits for them, and re-layouts  9.93 us (19%)
    pallas_call x1, Pallas kernels, local(): pl.pallas_call(functools.partial(block_kernel, n, rows_a, rows_b), out_sh...  42.5 us
    reshape x4, local copies, waits for them, and re-layouts, local(): row = lambda v: v.reshape(1, channels)  5.06 us
    unnamed x2, local copies, waits for them, and re-layouts  3.23 us
    pallas_call x1, local copies, waits for them, and re-layouts, local(): pl.pallas_call(functools.partial(block_kernel, n, rows_a, rows_b), out_sh...  1.63 us

profile of v1, /device:TPU:3, one launch (start us, length us, event | category | flops | bytes accessed | tf_op | source)
XLA Modules:
  0.0 52.4 jit_solution(11557409677479337847)
XLA Ops:
  0.0 1.2 %reshape.12.conv_bias = f32[1,320]{1,0:T(1,128)} reshape(f32[320]{0:T(512)} %param.17) | data formatting | bytes 2560 | tf_op jit(solution)/shard_map/reshape | solution.py:267
  1.2 1.3 %reshape.13.zero_bias = f32[1,320]{1,0:T(1,128)} reshape(f32[320]{0:T(512)} %param.19) | data formatting | bytes 2560 | tf_op jit(solution)/shard_map/reshape | solution.py:267
  2.5 1.3 %reshape.14.group_gain = f32[1,320]{1,0:T(1,128)} reshape(f32[320]{0:T(512)} %param.20) | data formatting | bytes 2560 | tf_op jit(solution)/shard_map/reshape | solution.py:267
  3.8 1.3 %reshape.15.norm_gain = f32[1,320]{1,0:T(1,128)} reshape(f32[320]{0:T(512)} %param.22) | data formatting | bytes 2560 | tf_op jit(solution)/shard_map/reshape | solution.py:267
  5.1 1.6 %copy.15.features = bf16[128,320]{1,0:T(8,128)(2,1)} copy(bf16[128,320]{0,1:T(8,128)(2,1)} %param.14) | data formatting | bytes 163840 | tf_op args[0]
  6.7 1.6 %copy.16.hint = bf16[128,320]{1,0:T(8,128)(2,1)} copy(bf16[128,320]{0,1:T(8,128)(2,1)} %param.15) | data formatting | bytes 163840 | tf_op args[1]
  8.3 42.5 %shard_map.136 = bf16[128,320]{1,0:T(8,128)(2,1)} custom-call(bf16[128,320]{1,0:T(8,128)(2,1)} %copy.15.features, bf16[128,320]{1,0:T(8,128)(2,1)} %copy.16.hint, f32[1,320]{1,0:T(1,128)} %reshape.12.conv_bias, f32[1,320]{1,0:T(1,128)} %reshape.13.zero_bias, f32[1,320]{1,0:T(1,128)} %reshape.14.group_gain, f32[1,320]{1,0:T(1,128)} %reshape.15.norm_gain, ...), custom_call_target="tpu_custom_call" | custom-call | tf_op jit(solution)/shard_map/pallas_call | solution.py:268
  50.8 1.6 %copy.17 = bf16[128,320]{0,1:T(8,128)(2,1)} copy(bf16[128,320]{1,0:T(8,128)(2,1)} %shard_map.136) | data formatting | bytes 163840 | tf_op jit(solution)/shard_map/pallas_call | solution.py:268

commit v2 on v1

v2 whole, which is shorter than its diff:
```python
import functools
import math

import jax
import jax.numpy as jnp
from jax import lax
from jax.experimental import pallas as pl
from jax.experimental.pallas import tpu as pltpu
from jax.sharding import PartitionSpec as P

HEADS = 8
GROUPS = 32
WIDTH = 128
CORES = 2

norm_eps = 1e-06
layer_eps = 1e-05
MESH = pl.DeviceIdType.MESH
F32 = jnp.float32
BF16 = jnp.bfloat16


def mm(x, y):
    return jnp.dot(x, y, preferred_element_type=F32)


def block_kernel(
    n, rows_a, rows_b,
    features, hint, conv_bias, zero_bias, group_gain, norm_gain,
    conv_hbm, zero_hbm, proj_in_hbm, query_hbm, key_hbm, value_hbm, attn_hbm, proj_hbm,
    out,
    conv_w, zero_w, proj_in_w, query_w, key_w, value_w, attn_w, proj_w,
    ext, gathered, keys_all, keys_t, qmask, scores, mixed,
    load_sem, halo_send, halo_recv, send_sem, recv_sem,
):
    channels, tokens = features.shape
    head_dim = channels // HEADS
    per_group = channels // GROUPS
    me = lax.axis_index("seq")
    core = lax.rem(me, CORES)
    chip = lax.div(me, CORES)
    b = lax.rem(chip, rows_b)
    a = lax.div(chip, rows_b)

    def device(aa, bb, cc):
        return (aa * rows_b + bb) * CORES + cc

    def as_columns(vector):
        return jnp.transpose(jnp.broadcast_to(vector[...].reshape(1, channels), (WIDTH, channels)))[:, :1]

    loads = {}
    for slot, (name, src, dst) in enumerate((
        ("conv", conv_hbm, conv_w), ("zero", zero_hbm, zero_w), ("proj_in", proj_in_hbm, proj_in_w),
        ("query", query_hbm, query_w), ("key", key_hbm, key_w), ("value", value_hbm, value_w),
        ("attn", attn_hbm, attn_w), ("proj", proj_hbm, proj_w),
    )):
        loads[name] = pltpu.make_async_copy(src, dst, load_sem.at[slot])
        loads[name].start()

    barrier = pltpu.get_barrier_semaphore()
    always = jnp.int32(1)
    peers = [
        (me > 0, me - 1), (me < n - 1, me + 1),
        (a > 0, device(a - 1, b, core)), (a < rows_a - 1, device(a + 1, b, core)),
        (None, device(a, b, 1 - core)),
    ]
    for k in range(1, rows_b):
        peers.append((None, device(a, lax.rem(b + k, rows_b), core)))
    count = jnp.int32(0)
    for cond, peer in peers:
        def greet(peer=peer):
            pl.semaphore_signal(barrier, inc=1, device_id={"seq": peer}, device_id_type=MESH)
        if cond is None:
            greet()
            count = count + always
        else:
            pl.when(cond)(greet)
            count = count + cond.astype(jnp.int32)
    pl.semaphore_wait(barrier, count)

    to_next = pltpu.make_async_remote_copy(
        hint.at[:, pl.ds(tokens - WIDTH, WIDTH)], ext.at[:, pl.ds(0, WIDTH)],
        halo_send.at[0], halo_recv.at[0], device_id={"seq": me + 1}, device_id_type=MESH)
    to_prev = pltpu.make_async_remote_copy(
        hint.at[:, pl.ds(0, WIDTH)], ext.at[:, pl.ds(WIDTH + tokens, WIDTH)],
        halo_send.at[1], halo_recv.at[1], device_id={"seq": me - 1}, device_id_type=MESH)
    pl.when(me < n - 1)(to_next.start)
    pl.when(me > 0)(to_prev.start)

    ext[:, pl.ds(WIDTH, tokens)] = hint[...]

    @pl.when(me == 0)
    def _():
        ext[:, pl.ds(0, WIDTH)] = jnp.zeros((channels, WIDTH), BF16)

    @pl.when(me == n - 1)
    def _():
        ext[:, pl.ds(WIDTH + tokens, WIDTH)] = jnp.zeros((channels, WIDTH), BF16)

    middle = jnp.transpose(hint[...])
    loads["conv"].wait()
    taps = [mm(middle, conv_w[1, d]) for d in range(3)]
    pl.when(me > 0)(to_next.wait_recv)
    pl.when(me < n - 1)(to_prev.wait_recv)
    for dy in (0, 2):
        lines = jnp.transpose(ext[:, pl.ds(dy * WIDTH, tokens)])
        taps = [taps[d] + mm(lines, conv_w[dy, d]) for d in range(3)]
    column = lax.rem(lax.broadcasted_iota(jnp.int32, (tokens, channels), 0), WIDTH)
    left = jnp.where(column == 0, 0.0, pltpu.roll(taps[0], 1, 0))
    right = jnp.where(column == WIDTH - 1, 0.0, pltpu.roll(taps[2], tokens - 1, 0))
    conv = left + taps[1] + right + conv_bias[...].reshape(1, channels)
    control = (conv / (1.0 + jnp.exp(-conv))).astype(BF16)
    loads["zero"].wait()
    branch = mm(control, zero_w[...]) + zero_bias[...].reshape(1, channels)
    merged = (features[...].astype(F32) + jnp.transpose(branch)).astype(BF16)
    gathered[me] = merged

    pending = []

    def send(src, target, cond):
        slot = len(pending)
        copy = pltpu.make_async_remote_copy(
            gathered.at[src], gathered.at[src], send_sem.at[slot], recv_sem.at[src],
            device_id={"seq": target}, device_id_type=MESH)
        pending.append((cond, copy))
        if cond is None:
            copy.start()
        else:
            pl.when(cond)(copy.start)

    def arrive(src, cond):
        def wait():
            pltpu.make_async_remote_copy(
                gathered.at[src], gathered.at[src], send_sem.at[0], recv_sem.at[src],
                device_id={"seq": me}, device_id_type=MESH).wait_recv()
        if cond is None:
            wait()
        else:
            pl.when(cond)(wait)

    def both(first, second):
        return second if first is None else first & second

    def to_partner(src, cond):
        send(src, device(a, b, 1 - core), cond)

    def along_b(src, cond):
        for k in range(1, rows_b):
            send(src, device(a, lax.rem(b + k, rows_b), core), cond)

    def from_b(aa, cond):
        for k in range(1, rows_b):
            src = device(aa, lax.rem(b + k, rows_b), core)
            arrive(src, cond)
            yield src

    even, odd = core == 0, core == 1
    up, down = a < rows_a - 1, a > 0

    along_b(me, None)
    send(me, device(a + 1, b, core), up)
    send(me, device(a - 1, b, core), down)
    to_partner(me, None)

    for name in ("proj_in", "query", "key", "value", "attn", "proj"):
        loads[name].wait()
    for weight in (proj_in_w, query_w, value_w, attn_w, proj_w):
        weight[...] = jnp.transpose(weight[...])
    gain, layer_gain = as_columns(group_gain), as_columns(norm_gain)
    row_group = lax.div(lax.broadcasted_iota(jnp.int32, (channels, channels), 0), jnp.int32(per_group))
    col_group = lax.div(lax.broadcasted_iota(jnp.int32, (channels, channels), 1), jnp.int32(per_group))
    same = (row_group == col_group).astype(F32)

    def group_sum(partial):
        total = jnp.dot(same, partial, preferred_element_type=F32, precision=lax.Precision.HIGHEST)
        return jnp.sum(total, axis=1, keepdims=True)

    shift = group_sum(merged.astype(F32)) / (tokens * per_group)

    for src in from_b(a, None):
        send(src, device(a + 1, b, core), even & up)
        send(src, device(a - 1, b, core), even & down)
        to_partner(src, None)
    for step in range(1, rows_a):
        for sign, more in ((-1, up), (1, down)):
            aa = a + sign * step
            inside = (aa >= 0) & (aa < rows_a)
            src = device(aa, b, core)
            arrive(src, inside)
            send(src, device(a - sign, b, core), inside & more)
            along_b(src, inside & odd)
            to_partner(src, inside)
            for k in range(1, rows_b):
                src = device(aa, lax.rem(b + k, rows_b), core)
                arrive(src, inside & even)
                send(src, device(a - sign, b, core), inside & more & even)
                to_partner(src, inside & even)
        for sign in (-1, 1):
            aa = a + sign * step
            inside = (aa >= 0) & (aa < rows_a) & odd
            for src in from_b(aa, inside):
                to_partner(src, inside)

    def add_block(src, acc):
        apart = gathered[src].astype(F32) - shift
        return acc[0] + apart, acc[1] + apart * apart

    zero_acc = jnp.zeros((channels, tokens), F32)
    sums = lax.fori_loop(0, n // CORES, lambda k, acc: add_block(k * CORES + core, acc), (zero_acc, zero_acc))
    for k in range(n // CORES):
        arrive(k * CORES + 1 - core, None)
        sums = add_block(k * CORES + 1 - core, sums)
    entry_count = tokens * n * per_group
    apart_mean = group_sum(sums[0]) / entry_count
    mean = shift + apart_mean
    var = jnp.maximum(group_sum(sums[1]) / entry_count - apart_mean * apart_mean, 0.0)
    inv = lax.rsqrt(var + norm_eps) * gain

    def project_norm(block):
        grouped = ((block.astype(F32) - mean) * inv).astype(BF16)
        inner = mm(proj_in_w[...], grouped).astype(BF16).astype(F32)
        centred = inner - jnp.mean(inner, axis=0, keepdims=True)
        spread = jnp.mean(jnp.square(centred), axis=0, keepdims=True)
        return inner, (centred * lax.rsqrt(spread + layer_eps) * layer_gain).astype(BF16)

    inner_own, normed_own = project_norm(merged)
    chunk = 4 if n % 4 == 0 else 1

    def norm_chunk(k, carry):
        block = jnp.concatenate([gathered[k * chunk + i] for i in range(chunk)], axis=1)
        normed = project_norm(block)[1]
        start = pl.multiple_of(k * chunk * tokens, chunk * tokens)
        keys_t[:, pl.ds(start, chunk * tokens)] = normed
        keys_all[pl.ds(start, chunk * tokens)] = jnp.transpose(normed)
        return carry

    lax.fori_loop(0, n // chunk, norm_chunk, 0)

    queries = mm(query_w[...], normed_own)
    row_head = lax.div(lax.broadcasted_iota(jnp.int32, (channels, tokens), 0), jnp.int32(head_dim))
    for h in range(HEADS):
        qmask[:, h * tokens:(h + 1) * tokens] = jnp.where(row_head == h, queries, 0.0).astype(BF16)
    scale = math.log2(math.e) / math.sqrt(head_dim)
    qmask[...] = (mm(key_w[...], qmask[...]) * scale).astype(BF16)

    pair = 2 * tokens
    for h2 in range(HEADS // 2):
        cols = slice(h2 * pair, (h2 + 1) * pair)
        scores[...] = mm(keys_all[...], qmask[:, cols])
        top = jnp.max(scores[...], axis=0, keepdims=True)
        weights = jnp.exp2(scores[...] - top)
        total = jnp.sum(weights, axis=0, keepdims=True)
        folded = (mm(keys_t[...], weights.astype(BF16)) / total).astype(BF16)
        values = mm(value_w[...], folded)
        for j in range(2):
            h = 2 * h2 + j
            mixed[pl.ds(h * head_dim, head_dim)] = values[h * head_dim:(h + 1) * head_dim, j * tokens:(j + 1) * tokens]
    after = (inner_own + mm(attn_w[...], mixed[...].astype(BF16))).astype(BF16)
    out[...] = (merged.astype(F32) + mm(proj_w[...], after)).astype(BF16)

    pl.when(me < n - 1)(to_next.wait_send)
    pl.when(me > 0)(to_prev.wait_send)
    for cond, copy in pending:
        if cond is None:
            copy.wait_send()
        else:
            pl.when(cond)(copy.wait_send)


def local(
    n, features, hint, conv_weight, conv_bias, zero_weight, zero_bias, group_gain, proj_in,
    norm_gain, query_weight, key_weight, value_weight, attn_out, proj_out,
):
    tokens, channels = features.shape
    chips = n // CORES
    rows_a = math.gcd(chips, 4)
    rows_b = chips // rows_a
    sends = 2 + rows_b + 3 * (rows_b - 1) + (rows_a - 1) * 2 * (1 + rows_b + 3 * (rows_b - 1))
    square = pltpu.VMEM((channels, channels), BF16)
    vmem = pl.BlockSpec(memory_space=pltpu.VMEM)
    hbm = pl.BlockSpec(memory_space=pl.ANY)
    result = pl.pallas_call(
        functools.partial(block_kernel, n, rows_a, rows_b),
        out_shape=jax.ShapeDtypeStruct((channels, tokens), BF16),
        in_specs=[vmem] * 6 + [hbm] * 8,
        out_specs=vmem,
        scratch_shapes=[
            pltpu.VMEM(conv_weight.shape, BF16), square, square, square, square, square, square, square,
            pltpu.VMEM((channels, tokens + 2 * WIDTH), BF16),
            pltpu.VMEM((n, channels, tokens), BF16),
            pltpu.VMEM((n * tokens, channels), BF16),
            pltpu.VMEM((channels, n * tokens), BF16),
            pltpu.VMEM((channels, HEADS * tokens), BF16),
            pltpu.VMEM((n * tokens, 2 * tokens), F32),
            pltpu.VMEM((channels, tokens), F32),
            pltpu.SemaphoreType.DMA((8,)),
            pltpu.SemaphoreType.DMA((2,)),
            pltpu.SemaphoreType.DMA((2,)),
            pltpu.SemaphoreType.DMA((sends,)),
            pltpu.SemaphoreType.DMA((n,)),
        ],
        compiler_params=pltpu.CompilerParams(
            collective_id=0, has_side_effects=True, vmem_limit_bytes=60 * 1024 * 1024),
    )(features.T, hint.T, conv_bias, zero_bias, group_gain, norm_gain,
      conv_weight, zero_weight, proj_in, query_weight, key_weight, value_weight, attn_out, proj_out)
    return result.T


def solution(mesh):
    split = P(("dp", "seq"), None)
    return jax.shard_map(
        functools.partial(local, mesh.shape["seq"]), mesh=mesh,
        in_specs=(split, split) + (P(),) * 12, out_specs=split, check_vma=False,
    )
```

time: 52.8 us -> 42.3 us (0.80)
  the two profiles are of different devices: /device:TPU:3 before, /device:TPU:0 now
where the time goes in v2:
time: 42.3 us; the launch traced here: 42.1 us
  Pallas kernels  40.6 us (96%)
  local copies, waits for them, and re-layouts  1.53 us (4%)
    pallas_call x1, Pallas kernels, local(): pl.pallas_call(functools.partial(block_kernel, n, rows_a, rows_b), out_sh...  40.6 us
    unnamed x1, local copies, waits for them, and re-layouts  1.53 us

profile of v2, /device:TPU:0, one launch (start us, length us, event | category | flops | bytes accessed | tf_op | source)
XLA Modules:
  0.0 42.1 jit_solution(9401823892519177815)
XLA Ops:
  0.0 40.6 %shard_map.136 = bf16[320,128]{1,0:T(8,128)(2,1)} custom-call(bf16[320,128]{1,0:T(8,128)(2,1)} %bitcast.4, bf16[320,128]{1,0:T(8,128)(2,1)} %bitcast.5, f32[320]{0:T(512)} %conv_bias.1, f32[320]{0:T(512)} %zero_bias.1, f32[320]{0:T(512)} %group_gain.1, f32[320]{0:T(512)} %norm_gain.1, bf16[3,3,320,320]{3,2,1,0:T(8,128)(2,1)} %conv_hbm.1, ...), custom_call_target="tpu_custom_call" | custom-call | tf_op jit(solution)/shard_map/pallas_call | solution.py:282
  40.6 1.5 %copy.16 = bf16[128,320]{0,1:T(8,128)(2,1)} copy(bf16[128,320]{0,1:T(8,128)(2,1)} %bitcast.3) | data formatting | bytes 163840

commit v3 on v2

--- a/solution.py
+++ b/solution.py
@@ -244,11 +244,15 @@
     qmask[...] = (mm(key_w[...], qmask[...]) * scale).astype(BF16)
 
     pair = 2 * tokens
+    def score(h2):
+        scores[h2 % 2] = mm(keys_all[...], qmask[:, h2 * pair:(h2 + 1) * pair])
+
+    score(0)
     for h2 in range(HEADS // 2):
-        cols = slice(h2 * pair, (h2 + 1) * pair)
-        scores[...] = mm(keys_all[...], qmask[:, cols])
-        top = jnp.max(scores[...], axis=0, keepdims=True)
-        weights = jnp.exp2(scores[...] - top)
+        if h2 + 1 < HEADS // 2:
+            score(h2 + 1)
+        top = jnp.max(scores[h2 % 2], axis=0, keepdims=True)
+        weights = jnp.exp2(scores[h2 % 2] - top)
         total = jnp.sum(weights, axis=0, keepdims=True)
         folded = (mm(keys_t[...], weights.astype(BF16)) / total).astype(BF16)
         values = mm(value_w[...], folded)
@@ -291,7 +295,7 @@
             pltpu.VMEM((n * tokens, channels), BF16),
             pltpu.VMEM((channels, n * tokens), BF16),
             pltpu.VMEM((channels, HEADS * tokens), BF16),
-            pltpu.VMEM((n * tokens, 2 * tokens), F32),
+            pltpu.VMEM((2, n * tokens, 2 * tokens), F32),
             pltpu.VMEM((channels, tokens), F32),
             pltpu.SemaphoreType.DMA((8,)),
             pltpu.SemaphoreType.DMA((2,)),

time: 42.3 us -> 38.8 us (0.917)
  Pallas kernels: 40.6 us -> 37.1 us
    pallas_call x1, Pallas kernels: 40.6 us -> 37.1 us  [local(): pl.pallas_call(functools.partial(block_kernel, n, rows_a, rows_b), out_sh...]
where the time goes in v3:
time: 38.8 us; the launch traced here: 38.6 us
  Pallas kernels  37.1 us (96%)
  local copies, waits for them, and re-layouts  1.53 us (4%)
    pallas_call x1, Pallas kernels, local(): pl.pallas_call(functools.partial(block_kernel, n, rows_a, rows_b), out_sh...  37.1 us
    unnamed x1, local copies, waits for them, and re-layouts  1.53 us

profile of v3, /device:TPU:0, one launch (start us, length us, event | category | flops | bytes accessed | tf_op | source)
XLA Modules:
  0.0 38.6 jit_solution(15618462230706256747)
XLA Ops:
  0.0 37.1 %shard_map.136 = bf16[320,128]{1,0:T(8,128)(2,1)} custom-call(bf16[320,128]{1,0:T(8,128)(2,1)} %bitcast.4, bf16[320,128]{1,0:T(8,128)(2,1)} %bitcast.5, f32[320]{0:T(512)} %conv_bias.1, f32[320]{0:T(512)} %zero_bias.1, f32[320]{0:T(512)} %group_gain.1, f32[320]{0:T(512)} %norm_gain.1, bf16[3,3,320,320]{3,2,1,0:T(8,128)(2,1)} %conv_hbm.1, ...), custom_call_target="tpu_custom_call" | custom-call | tf_op jit(solution)/shard_map/pallas_call | solution.py:286
  37.1 1.5 %copy.16 = bf16[128,320]{0,1:T(8,128)(2,1)} copy(bf16[128,320]{0,1:T(8,128)(2,1)} %bitcast.3) | data formatting | bytes 163840
